TPU v7x, 32 devices: a whole 2x2x4 slice. The times are simulated.
32 devices in a mesh: dp: 2 (over x), tp: 4 (over z), sq: 4 (over y, core).
Axes of the slice: x: 2, y: 2, z: 4, core: 2. Of those that a mesh axis runs over, the one named last changes fastest.
Arguments:
- hidden: bfloat16 [512, 2048], P('dp'), parts along dimension 0
- cache_lens: int32 [512], P('dp'), parts along dimension 0
- k_cache: bfloat16 [512, 1024, 128], P('dp', 'sq'), parts along dimension 0
- v_cache: bfloat16 [512, 1024, 128], P('dp', 'sq'), parts along dimension 0
- ln_gain: float32 [2048], replicated
- ln_bias: float32 [2048], replicated
- w_query: bfloat16 [2048, 2048], P(None, 'tp')
- b_query: float32 [2048], P('tp')
- w_kv: bfloat16 [2048, 256], replicated
- b_kv: float32 [256], replicated
- w_out: bfloat16 [2048, 2048], P('tp')
- b_out: float32 [2048], replicated
Outputs:
- output 1: bfloat16 [512, 2048], P('dp'), parts along dimension 0
- output 2: bfloat16 [512, 1024, 128], P('dp', 'sq'), parts along dimension 0
- output 3: bfloat16 [512, 1024, 128], P('dp', 'sq'), parts along dimension 0
There are 2 independent parts. A program takes and returns all parts, laid end to end along the dimension named above; an argument that names none is the same for every part.
All inputs are finite; a program needn't handle non-finite values.
Results may differ from a plain program's by a relative error of at most 0.00347619.
Values sent between devices are 32-bit elements.
A program may use at most 1 GiB of HBM per device.

v0:
```python
import functools

import jax
import jax.numpy as jnp
from jax import lax
from jax.experimental import pallas as pl
from jax.experimental.pallas import tpu as pltpu
from jax.sharding import PartitionSpec as P

F32 = jnp.float32
BF16 = jnp.bfloat16
NEG = -1e30


def attend_kernel(
    pairs, held, lens_ref, x_hbm, gain_ref, bias_ref, wq_hbm, bq_ref, wkv_hbm, bkv_ref, k_hbm, v_hbm,
    k_out, v_out, acc_out,
    x_buf, h_buf, wq_buf, wkv_buf, q_buf, kv_buf, s_buf, acc_ref, ml_ref, k_buf, v_buf,
    in_sem, k_sem, v_sem, ko_sem, vo_sem, acc_sem, ml_sem,
):
    batch, pos_local, dim = k_buf.shape
    heads = wq_buf.shape[1] // dim
    per = 2 * pairs
    chunks = batch // per
    rows = 2 * heads
    first_pos = lax.axis_index("sq") * pos_local
    scale = dim ** -0.5

    x_copy = pltpu.make_async_copy(x_hbm, x_buf, in_sem.at[0])
    kv_copy = pltpu.make_async_copy(wkv_hbm, wkv_buf, in_sem.at[1])
    q_copy = pltpu.make_async_copy(wq_hbm, wq_buf, in_sem.at[2])
    x_copy.start()
    kv_copy.start()
    q_copy.start()

    def span(ref, c):
        return ref.at[pl.ds(c * per, per)]

    def k_load(c):
        return pltpu.make_async_copy(span(k_hbm, c), span(k_buf, c), k_sem.at[c])

    def v_load(c):
        return pltpu.make_async_copy(span(v_hbm, c), span(v_buf, c), v_sem.at[c])

    def k_store(c):
        return pltpu.make_async_copy(span(k_buf, c), span(k_out, c), ko_sem.at[c])

    def v_store(c):
        return pltpu.make_async_copy(span(v_buf, c), span(v_out, c), vo_sem.at[c])

    @pl.loop(0, chunks)
    def _(c):
        k_load(c).start()
        v_load(c).start(priority=1)

    x_copy.wait()
    block = 32

    @pl.loop(0, batch // block)
    def _(i):
        x = x_buf[pl.ds(i * block, block), :].astype(F32)
        mean = jnp.mean(x, axis=-1, keepdims=True)
        cen = x - mean
        var = jnp.mean(cen * cen, axis=-1, keepdims=True)
        h = cen * lax.rsqrt(var + 1e-5) * gain_ref[...] + bias_ref[...]
        h_buf[pl.ds(i * block, block), :] = h.astype(BF16)

    kv_copy.wait()
    kv = jnp.dot(h_buf[...], wkv_buf[...], preferred_element_type=F32) + bkv_ref[...]
    kv_buf[...] = kv.astype(BF16).astype(F32)
    q_copy.wait()
    for n0 in range(0, heads, 2):
        cols = slice(n0 * dim, (n0 + 2) * dim)
        q = jnp.dot(h_buf[...], wq_buf[:, cols], preferred_element_type=F32) + bq_ref[:, cols]
        q = q.astype(BF16).astype(F32)
        q_buf[pl.ds(n0, batch, stride=heads), :] = q[:, :dim]
        q_buf[pl.ds(n0 + 1, batch, stride=heads), :] = q[:, dim:]

    top = lax.broadcasted_iota(jnp.int32, (rows, dim), 0) < heads
    top2 = lax.broadcasted_iota(jnp.int32, (rows, pos_local), 0) < heads
    lane = lax.broadcasted_iota(jnp.int32, (rows, dim), 1)
    place = first_pos + lax.broadcasted_iota(jnp.int32, (rows, pos_local), 1)
    sub = lax.broadcasted_iota(jnp.int32, (16, dim), 0)

    def update_rows(c):
        fresh = kv_buf[pl.ds(pl.multiple_of(c * per, per), per), :]
        for j in range(per):
            b = c * per + j
            at = lens_ref[b] - first_pos
            base = pl.multiple_of(jnp.clip(at, 0, pos_local - 1) // 16 * 16, 16)
            hit = sub == at - base
            for buf, lo in ((k_buf, 0), (v_buf, dim)):
                new = jnp.broadcast_to(fresh[j:j + 1, lo:lo + dim], (16, dim))
                old = buf[b, pl.ds(base, 16), :].astype(F32)
                buf[b, pl.ds(base, 16), :] = jnp.where(hit, new, old).astype(BF16)

    def score(c):
        out = []
        for j in range(pairs):
            p = c * pairs + j
            q = q_buf[pl.ds(pl.multiple_of(p * rows, rows), rows), :]
            lhs = jnp.concatenate([jnp.where(top, q, 0.0), jnp.where(top, 0.0, q)], axis=1).astype(BF16)
            keys = jnp.concatenate([k_buf[2 * p], k_buf[2 * p + 1]], axis=1)
            s = lax.dot_general(lhs, keys, (((1,), (1,)), ((), ())), preferred_element_type=F32)
            out.append(s)
        return out

    def weigh(c, m_all, l_all):
        for j in range(pairs):
            p = c * pairs + j
            s = s_buf[j * rows:(j + 1) * rows, :] * scale
            last = jnp.where(top2, lens_ref[2 * p], lens_ref[2 * p + 1])
            valid = place <= last
            s = jnp.where(valid, s, NEG)
            m = jnp.max(s, axis=-1, keepdims=True)
            w = jnp.where(valid, jnp.exp(s - m), 0.0)
            total = jnp.sum(w, axis=-1, keepdims=True)
            vals = jnp.concatenate([v_buf[2 * p], v_buf[2 * p + 1]], axis=1)
            o = jnp.dot(w.astype(BF16), vals, preferred_element_type=F32)
            acc_ref[pl.ds(pl.multiple_of(p * rows, rows), rows), :] = jnp.where(top, o[:, :dim], o[:, dim:])
            m_all = jnp.where(lane == p, m, m_all)
            l_all = jnp.where(lane == p, total, l_all)
        return m_all, l_all

    def put_scores(out):
        for j, s in enumerate(out):
            s_buf[j * rows:(j + 1) * rows, :] = s

    def acc_store(c):
        part = pl.ds(pl.multiple_of(c * (pairs * rows), pairs * rows), pairs * rows)
        return pltpu.make_async_copy(acc_ref.at[part], acc_out.at[part], acc_sem.at[c])

    def loaded(c):
        k_load(c).wait()
        v_load(c).wait()

    def leave(c):
        k_store(c).start()
        v_store(c).start(priority=1)

    loaded(0)
    update_rows(0)
    put_scores(score(0))
    zero = jnp.zeros((rows, dim), F32)

    def early(c, carry):
        loaded(c + 1)
        update_rows(c + 1)
        carry = weigh(c, *carry)
        put_scores(score(c + 1))
        acc_store(c).start()
        return carry

    carry = lax.fori_loop(0, held, early, (zero, zero))

    @pl.loop(held + 1, chunks)
    def _(c):
        loaded(c)

    @pl.loop(0, held + 1)
    def _(c):
        leave(c)

    def late(c, carry):
        update_rows(c + 1)
        carry = weigh(c, *carry)
        put_scores(score(c + 1))
        acc_store(c).start()
        leave(c + 1)
        return carry

    carry = lax.fori_loop(held, chunks - 1, late, carry)
    m_all, l_all = weigh(chunks - 1, *carry)
    ml_ref[:rows, :] = m_all
    ml_ref[rows:, :] = l_all
    acc_store(chunks - 1).start()

    @pl.loop(0, chunks - 1)
    def _(c):
        k_store(c).wait()
        v_store(c).wait()
        acc_store(c).wait()

    ml_store = pltpu.make_async_copy(ml_ref, acc_out.at[pl.ds(batch * heads, 2 * rows)], ml_sem)
    ml_store.start()
    k_store(chunks - 1).wait()
    v_store(chunks - 1).wait()
    acc_store(chunks - 1).wait()
    ml_store.wait()


def attend(lens, x, gain, bias, wq, bq, wkv, bkv, k, v, pairs=8, held=6):
    batch, pos_local, dim = k.shape
    width = x.shape[1]
    heads = wq.shape[1] // dim
    chunks = batch // (2 * pairs)
    hbm = pl.BlockSpec(memory_space=pltpu.HBM)
    vmem = pl.BlockSpec(memory_space=pltpu.VMEM)
    dma = pltpu.SemaphoreType.DMA
    return pl.pallas_call(
        functools.partial(attend_kernel, pairs, held),
        out_shape=(
            jax.ShapeDtypeStruct(k.shape, k.dtype),
            jax.ShapeDtypeStruct(v.shape, v.dtype),
            jax.ShapeDtypeStruct((batch * heads + 4 * heads, dim), F32),
        ),
        in_specs=[pl.BlockSpec(memory_space=pltpu.SMEM), hbm, vmem, vmem, hbm, vmem, hbm, vmem, hbm, hbm],
        out_specs=(hbm, hbm, hbm),
        scratch_shapes=[
            pltpu.VMEM(x.shape, BF16),
            pltpu.VMEM(x.shape, BF16),
            pltpu.VMEM(wq.shape, BF16),
            pltpu.VMEM(wkv.shape, BF16),
            pltpu.VMEM((batch * heads, dim), F32),
            pltpu.VMEM((batch, 2 * dim), F32),
            pltpu.VMEM((pairs * 2 * heads, pos_local), F32),
            pltpu.VMEM((batch * heads, dim), F32),
            pltpu.VMEM((4 * heads, dim), F32),
            pltpu.VMEM(k.shape, BF16),
            pltpu.VMEM(v.shape, BF16),
            dma((3,)), dma((chunks,)), dma((chunks,)), dma((chunks,)), dma((chunks,)), dma((chunks,)), dma,
        ],
        compiler_params=pltpu.CompilerParams(vmem_limit_bytes=60 * 1024 * 1024),
        cost_estimate=pl.CostEstimate(flops=2 * 2**30, bytes_accessed=72 * 2**20, transcendentals=0),
        name="attend",
    )(lens, x, gain.reshape(1, width), bias.reshape(1, width), wq, bq.reshape(1, -1), wkv, bkv.reshape(1, -1), k, v)


def meet_kernel(
    n_sq, parts, relayed, acc_hbm, x_hbm, wo_ref, bo_ref, out_ref,
    acc_buf, x_buf, base_buf, pair_buf, ml_pair, up_buf, ml_up, cross_buf, ml_cross, a_buf, z_out, far_in, in_buf, y_buf,
    in_sem, ml_send, ml_recv, mlu_send, mlu_recv, pair_send, pair_recv, up_send, up_recv, z_send, m_recv, s_recv, g_send, g_recv, y_send, y_recv, c_send, c_recv, f_send, f_recv,
):
    n_tp = z_out.shape[1]
    width = y_buf.shape[1]
    dim = acc_buf.shape[1]
    sq, tp = lax.axis_index("sq"), lax.axis_index("tp")
    own = y_buf.shape[0] // n_sq
    step = own // parts
    cols = width // n_tp
    heads = wo_ref.shape[0] // dim
    rows = 2 * heads
    pairs = step // 2
    fold = step * heads
    mesh_id = pl.DeviceIdType.MESH

    def at_tp(d):
        return {"tp": lax.rem(tp + d, n_tp)}

    core_sq = sq + 1 - 2 * lax.rem(sq, 2)
    across_sq = lax.rem(sq + 2, n_sq)
    core, across = {"sq": core_sq}, {"sq": across_sq}

    acc_in = pltpu.make_async_copy(acc_hbm, acc_buf, in_sem.at[0])
    acc_in.start()
    barrier = pltpu.get_barrier_semaphore()
    for to in (core, across):
        pl.semaphore_signal(barrier, inc=1, device_id=to, device_id_type=mesh_id)
    for d in range(1, n_tp):
        pl.semaphore_signal(barrier, inc=1, device_id=at_tp(d), device_id_type=mesh_id)
    x_cols = pl.ds(pl.multiple_of(tp * cols, cols), cols)
    x_in = pltpu.make_async_copy(x_hbm.at[pl.ds(pl.multiple_of(sq * own, own), own), x_cols], x_buf, in_sem.at[1])
    x_in.start()
    ml_own = acc_buf.at[pl.ds(own * n_sq * heads, 2 * rows)]
    with jax.named_scope('barrier'):
        acc_in.wait()
        pl.semaphore_wait(barrier, 2 + n_tp - 1)

    def remote(src, dst, send, recv, to):
        return pltpu.make_async_remote_copy(src_ref=src, dst_ref=dst, send_sem=send, recv_sem=recv, device_id=to, device_id_type=mesh_id)

    def acc_rows(s, c):
        return pl.ds(pl.multiple_of(s * (own * heads) + c * fold, fold), fold)

    def pair_copy(k, c):
        rows_for = acc_rows(core_sq if k == 0 else lax.rem(core_sq + 2, n_sq), c)
        return remote(acc_buf.at[rows_for], pair_buf.at[k, c], pair_send, pair_recv.at[k, c], core)

    def up_copy(c):
        return remote(up_buf.at[c], cross_buf.at[c], up_send, up_recv.at[c], across)

    ml_copy = remote(ml_own, ml_pair, ml_send, ml_recv, core)
    mlu_copy = remote(ml_up, ml_cross, mlu_send, mlu_recv, across)

    half = n_tp // 2
    middle = lax.div(tp + 1, 2) == 1
    partner = tp + 1 - 2 * lax.rem(tp, 2)
    far = half - half * lax.div(tp, half)

    def m_copy(c):
        return remote(z_out.at[c, pl.ds(far, half)], far_in.at[c], z_send, m_recv.at[c], {"tp": partner})

    def n_copy(c):
        return remote(z_out.at[c, partner], in_buf.at[c, 0], z_send, s_recv.at[c], {"tp": partner})

    def s_copy(k, c):
        return remote(z_out.at[c, far + k], in_buf.at[c, 1], z_send, s_recv.at[c], {"tp": far + k})

    def block(s, t, c):
        return y_buf.at[pl.ds(pl.multiple_of(s * own + c * step, step), step), pl.ds(pl.multiple_of(t * cols, cols), cols)]

    def source(tag):
        return tp - tag if tag < n_tp else tp + (tag - n_tp + 1)

    def source_of(tag, c):
        return source(tag) if c < relayed else lax.rem(tp - tag + n_tp, n_tp)

    def tp_copy(t, c, to):
        b = block(sq, t, c)
        return remote(b, b, g_send, g_recv.at[t, c], {"tp": to})

    def y_copy(tag, c):
        t = source_of(tag, c)
        b = block(sq, t, c)
        return remote(b, b, y_send, y_recv.at[t, c], across)

    def c_copy(tag, c):
        b = block(sq, source_of(tag, c), c)
        return remote(b, b, c_send, c_recv, core)

    def f_copy(tag, c):
        b = block(across_sq, source_of(tag, c), c)
        return remote(b, b, f_send, f_recv, core)

    def all_of(ref, send, recv):
        return remote(ref, ref, send, recv, {"tp": tp})

    ml_copy.start()
    for k in (1, 0):
        for c in range(parts):
            pair_copy(k, c).start()

    lane = lax.broadcasted_iota(jnp.int32, (rows, dim), 1)

    def column(e, p):
        return jnp.sum(jnp.where(lane == p, e, 0.0), axis=1, keepdims=True)

    def part_of(j):
        return slice(j * rows, (j + 1) * rows)

    with jax.named_scope("pairwait"):
        ml_copy.wait_recv()
    ml_at = own * n_sq * heads
    m_own, l_own = acc_buf[ml_at:ml_at + rows, :], acc_buf[ml_at + rows:ml_at + 2 * rows, :]
    m_pair, l_pair = ml_pair[:rows, :], ml_pair[rows:, :]
    m_up = jnp.maximum(m_own, m_pair)
    e_own, e_pair = jnp.exp(m_own - m_up), jnp.exp(m_pair - m_up)
    ml_up[:rows, :] = m_up
    ml_up[rows:, :] = e_own * l_own + e_pair * l_pair
    for c in range(parts):
        pair_copy(1, c).wait_recv()
        for j in range(pairs):
            p = across_sq * (own // 2) + c * pairs + j
            mine = pl.multiple_of(across_sq * (own * heads) + c * fold + j * rows, rows)
            up_buf[c, part_of(j), :] = column(e_own, p) * acc_buf[pl.ds(mine, rows), :] + column(e_pair, p) * pair_buf[1, c, part_of(j), :]
        if c == 0:
            mlu_copy.start()
        up_copy(c).start()

    x_in.wait()
    base_buf[...] = x_buf[...].astype(F32) + bo_ref[:, x_cols]
    with jax.named_scope("mlwait"):
        mlu_copy.wait_recv()
    m_cross, l_cross = ml_cross[:rows, :], ml_cross[rows:, :]
    top = jnp.maximum(m_up, m_cross)
    scales = [jnp.exp(m - top) for m in (m_own, m_pair, m_cross)]
    den = scales[0] * l_own + scales[1] * l_pair + scales[2] * l_cross
    scales = [e / den for e in scales]

    def when(cond):
        return pl.when(cond)

    def project(c):
        pair_copy(0, c).wait_recv()
        up_copy(c).wait_recv()
        for j in range(pairs):
            p = sq * (own // 2) + c * pairs + j
            mine = pl.multiple_of(sq * (own * heads) + c * fold + j * rows, rows)
            terms = (acc_buf[pl.ds(mine, rows), :], pair_buf[0, c, part_of(j), :], cross_buf[c, part_of(j), :])
            total = sum(column(e, p) * t for e, t in zip(scales, terms))
            a_buf[j * rows:(j + 1) * rows, :] = total
        lhs = jnp.concatenate([a_buf[pl.ds(n, step, stride=heads), :].astype(BF16) for n in range(heads)], axis=1)
        def term(t):
            w = wo_ref[:, pl.ds(pl.multiple_of(t * cols, cols), cols)]
            z_out[c, t] = jnp.dot(lhs, w, preferred_element_type=F32)

        for k in range(half):
            term(far + k)

        @when(jnp.logical_not(middle))
        def _():
            m_copy(c).start()

        term(partner)
        term(tp)

        if c:
            n_copy(c - 1).start()
        if c == parts - 1:
            n_copy(c).start()

    def add(c):
        @when(middle)
        def _():
            m_copy(c).wait_recv()
            for k in range(half):
                z_out[c, far + k] = z_out[c, far + k] + far_in[c, k]
            for k in range(half):
                s_copy(k, c).start()

    def share(tag, c):
        y_copy(tag, c).start()
        c_copy(tag, c).start()

    def finish(c):
        all_of(in_buf.at[c], z_send, s_recv.at[c]).wait_recv()
        total = z_out[c, tp] + in_buf[c, 0] + in_buf[c, 1]
        total = total + base_buf[c * step:(c + 1) * step, :]
        mine = block(sq, tp, c)
        mine[...] = total

        if c < relayed:
            @when(tp < n_tp - 1)
            def _():
                tp_copy(tp, c, tp + 1).start()

            @when(tp > 0)
            def _():
                tp_copy(tp, c, tp - 1).start()
        else:
            for d in range(1, n_tp):
                tp_copy(tp, c, lax.rem(tp + d, n_tp)).start()

        share(0, c)

    def direct(d, c):
        tp_copy(source_of(d, c), c, tp).wait_recv()
        share(d, c)

    def hop(h, c):
        @when(tp >= h)
        def _():
            tp_copy(tp - h, c, tp).wait_recv()

            @when(tp < n_tp - 1)
            def _():
                tp_copy(tp - h, c, tp + 1).start()

            share(h, c)

        @when(tp + h < n_tp)
        def _():
            tp_copy(tp + h, c, tp).wait_recv()

            @when(tp > 0)
            def _():
                tp_copy(tp + h, c, tp - 1).start()

            share(h + n_tp - 1, c)

    def crossed(h, c):
        def take(tag):
            y_copy(tag, c).wait_recv()
            f_copy(tag, c).start()

        if h == 0 or c >= relayed:
            take(h)
            return

        @when(tp >= h)
        def _():
            take(h)

        @when(tp + h < n_tp)
        def _():
            take(h + n_tp - 1)

    def named(name, fn, *args):
        def run():
            with jax.named_scope(name):
                fn(*args)
        return run

    events = []
    for c in range(parts):
        events.append((6.3 + 3.0 / parts * c, 0, named(f"p{c}", project, c)))
        events.append((8.1 + 8.4 / parts * (c + 1), 0, named(f"a{c}", add, c)))
        t = 11.7 + 8.4 / parts * (c + 1)
        events.append((t, 1, named(f"f{c}", finish, c)))
        events.append((t + 4.0, 3, named(f"y{c}_0", crossed, 0, c)))
        for h in range(1, n_tp):
            if c < relayed:
                there = t + 3.6 * h - 0.7
                events.append((there, 2, named(f"h{c}_{h}", hop, h, c)))
            else:
                there = t + 3.2 + 0.8 * h
                events.append((there, 2, named(f"d{c}_{h}", direct, h, c)))
            events.append((there + 5.0, 3, named(f"y{c}_{h}", crossed, h, c)))
    for _, _, event in sorted(events, key=lambda e: e[:2]):
        event()

    whole = y_buf.at[pl.ds(0, own)]
    with jax.named_scope("close"):
        all_of(whole, c_send, c_recv).wait()
        all_of(whole, f_send, f_recv).wait()
        all_of(whole, y_send, f_recv).wait_send()
        ml_copy.wait_send()
        mlu_copy.wait_send()
        all_of(pair_buf, pair_send, ml_recv).wait_send()
        all_of(up_buf, up_send, ml_recv).wait_send()
        all_of(z_out.at[:, pl.ds(0, half + 1)], z_send, ml_recv).wait_send()
        straight = (parts - relayed) * (n_tp - 1)

        @when(middle)
        def _():
            blocks = y_buf.at[pl.ds(0, (straight + relayed * (n_tp + 1)) * step // n_tp)]
            all_of(blocks, g_send, ml_recv).wait_send()

        @when(jnp.logical_not(middle))
        def _():
            blocks = y_buf.at[pl.ds(0, (straight + relayed) * step // n_tp)]
            all_of(blocks, g_send, ml_recv).wait_send()

    chunk = 32
    for i in range(y_buf.shape[0] // chunk):
      with jax.named_scope(f'emit{i}'):
        out_ref[i * chunk:(i + 1) * chunk, :] = y_buf[i * chunk:(i + 1) * chunk, :].astype(BF16)


def meet(acc, x, wo, bo, n_sq, n_tp, parts=4, relayed=2):
    batch, width = x.shape
    own = batch // n_sq
    cols = width // n_tp
    step = own // parts
    heads = wo.shape[0] // acc.shape[1]
    dim = acc.shape[1]
    vmem = pl.BlockSpec(memory_space=pltpu.VMEM)
    hbm = pl.BlockSpec(memory_space=pltpu.HBM)
    dma = pltpu.SemaphoreType.DMA
    return pl.pallas_call(
        functools.partial(meet_kernel, n_sq, parts, relayed),
        out_shape=jax.ShapeDtypeStruct((batch, width), BF16),
        in_specs=[hbm, hbm, vmem, vmem],
        out_specs=vmem,
        scratch_shapes=[
            pltpu.VMEM(acc.shape, F32),
            pltpu.VMEM((own, cols), BF16),
            pltpu.VMEM((own, cols), F32),
            pltpu.VMEM((2, parts, step * heads, dim), F32),
            pltpu.VMEM((4 * heads, dim), F32),
            pltpu.VMEM((parts, step * heads, dim), F32),
            pltpu.VMEM((4 * heads, dim), F32),
            pltpu.VMEM((parts, step * heads, dim), F32),
            pltpu.VMEM((4 * heads, dim), F32),
            pltpu.VMEM((step * heads, dim), F32),
            pltpu.VMEM((parts, n_tp, step, cols), F32),
            pltpu.VMEM((parts, n_tp // 2, step, cols), F32),
            pltpu.VMEM((parts, 2, step, cols), F32),
            pltpu.VMEM((batch, width), F32),
            dma((2,)), dma, dma, dma, dma, dma, dma((2, parts)), dma, dma((parts,)),
            dma, dma((parts,)), dma((parts,)), dma, dma((n_tp, parts)),
            dma, dma((n_tp, parts)), dma, dma, dma, dma,
        ],
        compiler_params=pltpu.CompilerParams(collective_id=0, has_side_effects=True, vmem_limit_bytes=32 * 1024 * 1024),
        cost_estimate=pl.CostEstimate(flops=2**28, bytes_accessed=8 * 2**20, transcendentals=0),
        name="meet",
    )(pltpu.with_memory_space_constraint(acc, pltpu.HBM), pltpu.with_memory_space_constraint(x, pltpu.HBM), wo, bo.reshape(1, width))


def solution(mesh):
    def local_step(hidden, cache_lens, k_cache, v_cache, ln_gain, ln_bias, w_query, b_query, w_kv, b_kv, w_out, b_out):
        key_new, val_new, acc = attend(
            cache_lens, hidden, ln_gain, ln_bias, w_query, b_query, w_kv, b_kv, k_cache, v_cache)
        out_hidden = meet(acc, hidden, w_out, b_out, mesh.shape["sq"], mesh.shape["tp"])
        return out_hidden, key_new, val_new

    cache_spec = P("dp", "sq", None)
    row_spec = P("dp", None)
    in_specs = (row_spec, P("dp"), cache_spec, cache_spec, P(None), P(None), P(None, "tp"), P("tp"), P(None, None), P(None), P("tp", None), P(None))
    out_specs = (row_spec, cache_spec, cache_spec)
    return jax.shard_map(local_step, mesh=mesh, in_specs=in_specs, out_specs=out_specs, check_vma=False)
```

profile of v0, /device:TPU:0, one launch (start us, length us, event | category | flops | bytes accessed | tf_op | source)
XLA Modules:
  0.0 61.9 jit_solution(85976363698308408)
XLA Ops:
  0.6 0.0 copy-start
  0.6 0.0 copy-start.1
  0.7 24.9 %attend.1 = (bf16[256,256,128]{2,1,0:T(8,128)(2,1)}, bf16[256,256,128]{2,1,0:T(8,128)(2,1)}, f32[1040,128]{1,0:T(8,128)}) custom-call(s32[256]{0:T(256)} %lens_ref.1, bf16[256,2048]{1,0:T(8,128)(2,1)} %x_hbm.3, f32[1,2048]{1,0:T(1,128)} %bitcast.6, f32[1,2048]{1,0:T(1,128)} %bitcast.7, bf16[2048,512]{1,0:T(8,128)(2,1)} %wq_hbm.1, f32[1,512]{1,0:T(1,128)} %bitcast.8, ...), custom_call_target="tpu_custom_call" | custom-call | flops 2147483648 | bytes 75497472 | tf_op jit(solution)/shard_map/attend/pallas_call | solution.py:200
  25.6 0.0 copy-done
  25.6 0.0 copy-done.1
  25.6 35.3 %meet.1 = bf16[256,2048]{1,0:T(8,128)(2,1)S(1)} custom-call(f32[1040,128]{1,0:T(8,128)} %get-tuple-element.6.acc_hbm, bf16[256,2048]{1,0:T(8,128)(2,1)} %x_hbm.3, bf16[512,2048]{1,0:T(8,128)(2,1)S(1)} %copy-done, f32[1,2048]{1,0:T(1,128)S(1)} %bitcast.5), custom_call_target="tpu_custom_call" | custom-call | flops 268435456 | bytes 8388608 | tf_op jit(solution)/shard_map/meet/pallas_call | solution.py:540
  60.9 1.0 %copy.16 = bf16[256,2048]{1,0:T(8,128)(2,1)} copy(bf16[256,2048]{1,0:T(8,128)(2,1)S(1)} %meet.1) | data formatting | bytes 2097152
Async XLA Ops:
  0.6 25.0 %copy-start = (bf16[512,2048]{1,0:T(8,128)(2,1)S(1)}, bf16[512,2048]{1,0:T(8,128)(2,1)}, u32[]{:S(2)}) copy-start(bf16[512,2048]{1,0:T(8,128)(2,1)} %wo_ref.1) | copy-start | bytes 6291460
  0.6 25.0 %copy-start.1 = (f32[2048]{0:T(1024)S(1)}, f32[2048]{0:T(1024)}, u32[]{:S(2)}) copy-start(f32[2048]{0:T(1024)} %param.23) | copy-start | bytes 24580
where the time goes:
time: 62 us; the launch traced here: 61.9 us
  Pallas kernels  60.2 us (97%)
  local copies, waits for them, and re-layouts  0.98 us (2%)
  between operations  0.68 us (1%)
    pallas_call x1, Pallas kernels, meet(): pl.pallas_call(functools.partial(meet_kernel, n_sq, parts, relayed), out_...  35.3 us
    pallas_call x1, Pallas kernels, attend(): pl.pallas_call(functools.partial(attend_kernel, pairs, held), out_shape=(...  24.9 us

commit v1 on v0

--- a/solution.py
+++ b/solution.py
@@ -493,7 +493,7 @@
                 there = t + 3.6 * h - 0.7
                 events.append((there, 2, named(f"h{c}_{h}", hop, h, c)))
             else:
-                there = t + 3.2 + 0.8 * h
+                there = max(t, 17.4) + 3.2 + 0.8 * h
                 events.append((there, 2, named(f"d{c}_{h}", direct, h, c)))
             events.append((there + 5.0, 3, named(f"y{c}_{h}", crossed, h, c)))
     for _, _, event in sorted(events, key=lambda e: e[:2]):
@@ -527,7 +527,7 @@
         out_ref[i * chunk:(i + 1) * chunk, :] = y_buf[i * chunk:(i + 1) * chunk, :].astype(BF16)
 
 
-def meet(acc, x, wo, bo, n_sq, n_tp, parts=4, relayed=2):
+def meet(acc, x, wo, bo, n_sq, n_tp, parts=4, relayed=1):
     batch, width = x.shape
     own = batch // n_sq
     cols = width // n_tp

time: 62 us -> 64 us (1.032)
  Pallas kernels: 60.2 us -> 62.1 us
    pallas_call x1, Pallas kernels: 35.3 us -> 37.2 us  [meet(): pl.pallas_call(functools.partial(meet_kernel, n_sq, parts, relayed), out_...]
where the time goes in v1:
time: 64 us; the launch traced here: 63.8 us
  Pallas kernels  62.1 us (97%)
  local copies, waits for them, and re-layouts  0.98 us (2%)
  between operations  0.68 us (1%)
    pallas_call x1, Pallas kernels, meet(): pl.pallas_call(functools.partial(meet_kernel, n_sq, parts, relayed), out_...  37.2 us
    pallas_call x1, Pallas kernels, attend(): pl.pallas_call(functools.partial(attend_kernel, pairs, held), out_shape=(...  24.9 us

profile of v1, /device:TPU:0, one launch (start us, length us, event | category | flops | bytes accessed | tf_op | source)
XLA Modules:
  0.0 63.8 jit_solution(11970154788309348869)
XLA Ops:
  0.6 0.0 copy-start
  0.6 0.0 copy-start.1
  0.7 24.9 %attend.1 = (bf16[256,256,128]{2,1,0:T(8,128)(2,1)}, bf16[256,256,128]{2,1,0:T(8,128)(2,1)}, f32[1040,128]{1,0:T(8,128)}) custom-call(s32[256]{0:T(256)} %lens_ref.1, bf16[256,2048]{1,0:T(8,128)(2,1)} %x_hbm.3, f32[1,2048]{1,0:T(1,128)} %bitcast.6, f32[1,2048]{1,0:T(1,128)} %bitcast.7, bf16[2048,512]{1,0:T(8,128)(2,1)} %wq_hbm.1, f32[1,512]{1,0:T(1,128)} %bitcast.8, ...), custom_call_target="tpu_custom_call" | custom-call | flops 2147483648 | bytes 75497472 | tf_op jit(solution)/shard_map/attend/pallas_call | solution.py:200
  25.6 0.0 copy-done
  25.6 0.0 copy-done.1
  25.6 37.2 %meet.1 = bf16[256,2048]{1,0:T(8,128)(2,1)S(1)} custom-call(f32[1040,128]{1,0:T(8,128)} %get-tuple-element.6.acc_hbm, bf16[256,2048]{1,0:T(8,128)(2,1)} %x_hbm.3, bf16[512,2048]{1,0:T(8,128)(2,1)S(1)} %copy-done, f32[1,2048]{1,0:T(1,128)S(1)} %bitcast.5), custom_call_target="tpu_custom_call" | custom-call | flops 268435456 | bytes 8388608 | tf_op jit(solution)/shard_map/meet/pallas_call | solution.py:540
  62.8 1.0 %copy.16 = bf16[256,2048]{1,0:T(8,128)(2,1)} copy(bf16[256,2048]{1,0:T(8,128)(2,1)S(1)} %meet.1) | data formatting | bytes 2097152
Async XLA Ops:
  0.6 25.0 %copy-start = (bf16[512,2048]{1,0:T(8,128)(2,1)S(1)}, bf16[512,2048]{1,0:T(8,128)(2,1)}, u32[]{:S(2)}) copy-start(bf16[512,2048]{1,0:T(8,128)(2,1)} %wo_ref.1) | copy-start | bytes 6291460
  0.6 25.0 %copy-start.1 = (f32[2048]{0:T(1024)S(1)}, f32[2048]{0:T(1024)}, u32[]{:S(2)}) copy-start(f32[2048]{0:T(1024)} %param.23) | copy-start | bytes 24580

commit v2 on v0

--- a/solution.py
+++ b/solution.py
@@ -527,7 +527,7 @@
         out_ref[i * chunk:(i + 1) * chunk, :] = y_buf[i * chunk:(i + 1) * chunk, :].astype(BF16)
 
 
-def meet(acc, x, wo, bo, n_sq, n_tp, parts=4, relayed=2):
+def meet(acc, x, wo, bo, n_sq, n_tp, parts=4, relayed=3):
     batch, width = x.shape
     own = batch // n_sq
     cols = width // n_tp

time: 62 us -> 63.1 us (1.018)
  Pallas kernels: 60.2 us -> 61.3 us
    pallas_call x1, Pallas kernels: 35.3 us -> 36.3 us  [meet(): pl.pallas_call(functools.partial(meet_kernel, n_sq, parts, relayed), out_...]
where the time goes in v2:
time: 63.1 us; the launch traced here: 62.9 us
  Pallas kernels  61.3 us (97%)
  local copies, waits for them, and re-layouts  0.98 us (2%)
  between operations  0.68 us (1%)
    pallas_call x1, Pallas kernels, meet(): pl.pallas_call(functools.partial(meet_kernel, n_sq, parts, relayed), out_...  36.3 us
    pallas_call x1, Pallas kernels, attend(): pl.pallas_call(functools.partial(attend_kernel, pairs, held), out_shape=(...  24.9 us

profile of v2, /device:TPU:0, one launch (start us, length us, event | category | flops | bytes accessed | tf_op | source)
XLA Modules:
  0.0 62.9 jit_solution(6445902182177629359)
XLA Ops:
  0.6 0.0 copy-start
  0.6 0.0 copy-start.1
  0.7 24.9 %attend.1 = (bf16[256,256,128]{2,1,0:T(8,128)(2,1)}, bf16[256,256,128]{2,1,0:T(8,128)(2,1)}, f32[1040,128]{1,0:T(8,128)}) custom-call(s32[256]{0:T(256)} %lens_ref.1, bf16[256,2048]{1,0:T(8,128)(2,1)} %x_hbm.3, f32[1,2048]{1,0:T(1,128)} %bitcast.6, f32[1,2048]{1,0:T(1,128)} %bitcast.7, bf16[2048,512]{1,0:T(8,128)(2,1)} %wq_hbm.1, f32[1,512]{1,0:T(1,128)} %bitcast.8, ...), custom_call_target="tpu_custom_call" | custom-call | flops 2147483648 | bytes 75497472 | tf_op jit(solution)/shard_map/attend/pallas_call | solution.py:200
  25.6 0.0 copy-done
  25.6 0.0 copy-done.1
  25.6 36.3 %meet.1 = bf16[256,2048]{1,0:T(8,128)(2,1)S(1)} custom-call(f32[1040,128]{1,0:T(8,128)} %get-tuple-element.6.acc_hbm, bf16[256,2048]{1,0:T(8,128)(2,1)} %x_hbm.3, bf16[512,2048]{1,0:T(8,128)(2,1)S(1)} %copy-done, f32[1,2048]{1,0:T(1,128)S(1)} %bitcast.5), custom_call_target="tpu_custom_call" | custom-call | flops 268435456 | bytes 8388608 | tf_op jit(solution)/shard_map/meet/pallas_call | solution.py:540
  61.9 1.0 %copy.16 = bf16[256,2048]{1,0:T(8,128)(2,1)} copy(bf16[256,2048]{1,0:T(8,128)(2,1)S(1)} %meet.1) | data formatting | bytes 2097152
Async XLA Ops:
  0.6 25.0 %copy-start = (bf16[512,2048]{1,0:T(8,128)(2,1)S(1)}, bf16[512,2048]{1,0:T(8,128)(2,1)}, u32[]{:S(2)}) copy-start(bf16[512,2048]{1,0:T(8,128)(2,1)} %wo_ref.1) | copy-start | bytes 6291460
  0.6 25.0 %copy-start.1 = (f32[2048]{0:T(1024)S(1)}, f32[2048]{0:T(1024)}, u32[]{:S(2)}) copy-start(f32[2048]{0:T(1024)} %param.23) | copy-start | bytes 24580
